TPU v7x, 32 devices: a whole 2x2x4 slice. The times are simulated.
32 devices in a mesh: sub: 16 (over z, y, x), crs: 2 (over core).
Axes of the slice: x: 2, y: 2, z: 4, core: 2. Of those that a mesh axis runs over, the one named last changes fastest.
Arguments:
- multipliers: float32 [16, 128, 512], P(None, ('sub', 'crs')), may hold values from -6 to 6
- own_modes: float32 [6, 128, 512], P(None, ('sub', 'crs')), may hold values from -0.75 to 0.75
- neighbour_modes: float32 [6, 128, 512], P(None, ('sub', 'crs')), may hold values from -0.75 to 0.75
- face_index: int32 [128, 512], P(('sub', 'crs')), may hold values from 0 to 5, as said below
- neighbour_list: int32 [128, 6], replicated, may hold values from 0 to 127, as said below
- coarse_factor: float32 [768, 768], P('sub', 'crs'), may hold values from -0.21875 to 0.21875
Outputs:
- projected: float32 [16, 128, 512], P(None, ('sub', 'crs'))
Inputs may be any that keep to these rules, and one draw needn't show every extreme that they name: `face_index`: the multipliers of each subdomain lie in 6 contiguous nonempty blocks, face 0 first and face 5 last. `neighbour_list`: subdomain s = (8 x + y) * 8 + z sits at (x, y, z) of a periodic grid of 2 x 8 x 8 subdomains; the 6 faces of each subdomain name its grid neighbours x plus 1, x minus 1, y plus or minus 1, z plus or minus 1 (periodic; along the first dimension both name the same subdomain), in an order that differs from subdomain to subdomain.
All inputs are finite; a program needn't handle non-finite values.
Results may differ from a plain program's by a relative error of at most 0.0001.
Values sent between devices are 32-bit elements; how exact they have to be, the bound alone decides.
No kernel may reach another device: no remote copies, remote signals or barrier semaphores. Data moves between devices by JAX's collectives and lax.ppermute only.
A program may use at most 64 MiB of HBM per device.

v0:
```python
import jax
import jax.numpy as jnp
from jax import lax
from jax.sharding import PartitionSpec as P


MODES = 6
NFACE = 6
COL_LEN = 2
NDIR = 6
NBLOCK = 4

HIGHEST = lax.Precision.HIGHEST


def all_sum(value, axis):
    peers = lax.axis_size(axis)
    if peers & (peers - 1):
        return lax.psum(value, axis)
    step = 1
    while step < peers:
        value = value + lax.ppermute(value, axis, [(i, i ^ step) for i in range(peers)])
        step *= 2
    return value


def parity(i):
    return bin(i).count("1") % 2


def crossed_sum(value):
    peers = lax.axis_size("sub")
    step = 1
    while step < peers:
        pairs = [(2 * i + c, 2 * (i ^ step) + 1 - c) for i in range(peers) for c in range(2)]
        value = value + lax.ppermute(value, ("sub", "crs"), pairs)
        step *= 2
    return value


def body(multipliers, own_modes, neighbour_modes, face_index, neighbour_list, coarse_factor):
    width_rhs, local_subs, _ = multipliers.shape
    crs_size = lax.axis_size("crs")
    sub_size = lax.axis_size("sub")
    crs_rank = lax.axis_index("crs")
    sub_rank = lax.axis_index("sub")
    group_subs = local_subs * crs_size
    row_len = sub_size // COL_LEN
    first_sub = (sub_rank * crs_size + crs_rank) * local_subs

    crossed = crs_size == 2 and sub_size & (sub_size - 1) == 0

    def ring(i, by):
        return i // row_len * row_len + (i + by) % row_len

    def fetched(source):
        pairs = []
        for i in range(sub_size):
            for c in range(crs_size):
                half = c ^ parity(i) if crossed else c
                pairs.append((source(i) * crs_size + half, i * crs_size + c))
        return lax.ppermute(coarse_factor, ("sub", "crs"), pairs)

    own_factor = coarse_factor
    if crossed:
        other = lax.ppermute(coarse_factor, "crs", [(0, 1), (1, 0)])
        own_factor = jnp.where(lax.population_count(sub_rank) % 2 == 1, other, coarse_factor)
    factors = [
        own_factor,
        fetched(lambda i: (i + row_len) % sub_size),
        fetched(lambda i: ring(i, 1)),
        fetched(lambda i: ring(i, -1)),
    ]

    local_ids = first_sub + lax.iota(jnp.int32, local_subs)
    first = local_ids // (row_len * group_subs)
    second = local_ids // group_subs % row_len
    third = local_ids % group_subs

    def place(a, b, c):
        return (a * row_len + b) * group_subs + c

    across = [
        place((first + 1) % COL_LEN, second, third),
        place(first, (second + 1) % row_len, third),
        place(first, (second + row_len - 1) % row_len, third),
        place(first, second, (third + 1) % group_subs),
        place(first, second, (third + group_subs - 1) % group_subs),
    ]
    local_nbrs = lax.dynamic_slice_in_dim(neighbour_list, first_sub, local_subs, 0)
    face_dir = jnp.zeros_like(local_nbrs)
    for which in range(NDIR - 2, -1, -1):
        face_dir = jnp.where(local_nbrs == across[which][:, None], which + 1, face_dir)
    point_dir = jnp.zeros_like(face_index)
    for which_face in range(NFACE):
        point_dir = jnp.where(
            face_index == which_face, face_dir[:, which_face : which_face + 1], point_dir
        )
    rows = [own_modes]
    for which in range(1, NDIR):
        rows.append(jnp.where((point_dir == which)[None], neighbour_modes, 0.0))
    rows = jnp.stack(rows)
    sums = jnp.einsum("dksm,rsm->rsdk", rows, multipliers, precision=HIGHEST)

    blocks = jnp.array([0, 1, 2, 3, 0, 0], jnp.int32)
    moves = jnp.array([0, 0, 0, 0, 1, group_subs - 1], jnp.int32)
    target_sub = (third[:, None] + moves[None]) % group_subs
    target = (blocks[None] * group_subs + target_sub)[:, :, None] * MODES + lax.iota(jnp.int32, MODES)
    wide = NBLOCK * group_subs * MODES
    chosen = (target.reshape(-1, 1) == lax.iota(jnp.int32, wide)[None]).astype(jnp.float32)

    coarse = jnp.dot(sums.reshape(width_rhs, -1), chosen, precision=HIGHEST)
    coarse = all_sum(coarse, "crs").reshape(width_rhs, NBLOCK, group_subs * MODES)
    panel = 0.0
    for which in range(NBLOCK):
        panel = panel + jnp.dot(coarse[:, which], factors[which], precision=HIGHEST)
    panel = crossed_sum(panel) if crossed else all_sum(panel, "sub")
    amps = jnp.concatenate(
        [jnp.einsum("rp,cp->rc", panel, f, precision=HIGHEST) for f in factors], axis=1
    )
    amps = all_sum(amps, "crs")
    near = jnp.einsum("rw,nw->rn", amps, chosen, precision=HIGHEST)
    near = near.reshape(width_rhs, local_subs, NDIR, MODES)
    return multipliers - jnp.einsum("rsdk,dksm->rsm", near, rows, precision=HIGHEST)


def solution(mesh):
    placed = (
        P(None, ("sub", "crs"), None),
        P(None, ("sub", "crs"), None),
        P(None, ("sub", "crs"), None),
        P(("sub", "crs"), None),
        P(),
        P("sub", "crs"),
    )
    return jax.shard_map(
        body, mesh=mesh, in_specs=placed, out_specs=P(None, ("sub", "crs"), None), check_vma=False
    )
```

profile of v0, /device:TPU:0, one launch (start us, length us, event | category | flops | bytes accessed | tf_op | source)
XLA Modules:
  0.0 36.8 jit_solution(1471385823631763017)
XLA Ops:
  0.0 0.0 copy-start.5
  0.0 0.0 copy-start.3
  0.1 0.6 %copy-done.5 = s32[128,6]{0,1:T(8,128)S(1)} copy-done((s32[128,6]{0,1:T(8,128)S(1)}, s32[128,6]{0,1:T(8,128)}, u32[]{:S(2)}) %copy-start.5) | copy-done | bytes 3096
  0.7 0.1 select_select_fusion.1
  0.8 0.0 copy-start.4
  0.8 0.7 %copy-done.4 = s32[4,512]{1,0:T(4,128)S(1)} copy-done((s32[4,512]{1,0:T(4,128)S(1)}, s32[4,512]{1,0:T(4,128)}, u32[]{:S(2)}) %copy-start.4) | copy-done | bytes 8216
  1.5 0.1 broadcast_compare_fusion.4
  1.6 0.0 copy-done.3
  1.6 0.0 copy-start
  1.6 0.8 %copy-done = f32[6,4,512]{2,1,0:T(4,128)S(1)} copy-done((f32[6,4,512]{2,1,0:T(4,128)S(1)}, f32[6,4,512]{2,1,0:T(4,128)}, u32[]{:S(2)}) %copy-start) | copy-done | bytes 49176
  2.5 0.0 copy-start.1
  2.5 0.8 %copy-done.1 = f32[16,4,512]{2,1,0:T(4,128)S(1)} copy-done((f32[16,4,512]{2,1,0:T(4,128)S(1)}, f32[16,4,512]{2,1,0:T(4,128)}, u32[]{:S(2)}) %copy-start.1) | copy-done | bytes 131096
  3.4 0.5 %convolution_bitcast_fusion.1 = f32[16,4,6,6]{0,3,2,1:T(8,128)S(1)} fusion(f32[6,6,4,512]{3,1,0,2:T(8,128)S(1)} %fusion.17, f32[16,4,512,1]{2,1,0,3:T(4,128)S(1)} %bitcast.78), kind=kOutput, calls=%fused_computation.2 | convolution fusion | flops 14155776 | bytes 435200 | tf_op jit(solution)/shard_map/dksm,rsm->rsdk/dot_general | solution.py:103
  3.9 0.0 copy-start.6
  3.9 0.0 copy-start.7
  4.0 0.0 copy-start.2
  4.0 0.6 %copy-done.6 = s32[6]{0:T(128)S(1)} copy-done((s32[6]{0:T(128)S(1)}, s32[6]{0:T(128)}, u32[]{:S(2)}) %copy-start.6) | copy-done | bytes 48
  4.6 0.0 copy-done.7
  4.6 0.1 fusion.21
  4.7 0.1 copy.35
  4.8 0.1 iota_add_fusion
  4.9 0.1 add.378
  5.0 0.3 fusion.4
  5.2 0.5 %collective-permute-start = (f32[16,192]{1,0:T(8,128)S(1)}, f32[16,192]{1,0:T(8,128)S(1)}, u32[]{:S(2)}, u32[]{:S(2)}) collective-permute-start(f32[16,192]{1,0:T(8,128)S(1)} %fusion.4), channel_id=1, source_target_pairs={{0,1},{1,0},{2,3},{3,2},{4,5},{5,4},{6,7},{7,6},{8,9},{9,8},{10,11... | collective-permute-start | bytes 36872 | tf_op jit(solution)/shard_map/ppermute | solution.py:22
  5.7 0.0 copy-done.2
  5.7 3.7 %collective-permute-start.2 = (f32[48,384]{1,0:T(8,128)S(1)}, f32[48,384]{1,0:T(8,128)S(1)}, u32[]{:S(2)}, u32[]{:S(2)}) collective-permute-start(f32[48,384]{1,0:T(8,128)S(1)} %copy-done.2), channel_id=1, source_target_pairs={{16,0},{17,1},{19,2},{18,3},{21,4},{20,5},{22,6},{23,7},{25,8},{24... | collective-permute-start | bytes 221192 | tf_op jit(solution)/shard_map/ppermute | solution.py:62
  9.4 3.2 %collective-permute-start.3 = (f32[48,384]{1,0:T(8,128)S(1)}, f32[48,384]{1,0:T(8,128)S(1)}, u32[]{:S(2)}, u32[]{:S(2)}) collective-permute-start(f32[48,384]{1,0:T(8,128)S(1)} %copy-done.2), channel_id=1, source_target_pairs={{2,0},{3,1},{5,2},{4,3},{7,4},{6,5},{8,6},{9,7},{11,8},{10,9},{12,... | collective-permute-start | bytes 221192 | tf_op jit(solution)/shard_map/ppermute | solution.py:62
  12.6 0.0 collective-permute-start.4
  12.6 0.4 collective-permute-start.1
  13.0 0.0 collective-permute-done
  13.0 0.1 reshape.218
  13.1 0.7 %collective-permute-done.2 = f32[48,384]{1,0:T(8,128)S(1)} collective-permute-done((f32[48,384]{1,0:T(8,128)S(1)}, f32[48,384]{1,0:T(8,128)S(1)}, u32[]{:S(2)}, u32[]{:S(2)}) %collective-permute-start.2) | collective-permute-done | bytes 73760 | tf_op jit(solution)/shard_map/ppermute | solution.py:62
  13.8 0.2 fusion.38
  14.0 1.0 %collective-permute-done.3 = f32[48,384]{1,0:T(8,128)S(1)} collective-permute-done((f32[48,384]{1,0:T(8,128)S(1)}, f32[48,384]{1,0:T(8,128)S(1)}, u32[]{:S(2)}, u32[]{:S(2)}) %collective-permute-start.3) | collective-permute-done | bytes 73760 | tf_op jit(solution)/shard_map/ppermute | solution.py:62
  15.0 0.2 fusion.39
  15.1 3.8 %collective-permute-done.4 = f32[48,384]{1,0:T(8,128)S(1)} collective-permute-done((f32[48,384]{1,0:T(8,128)S(1)}, f32[48,384]{1,0:T(8,128)S(1)}, u32[]{:S(2)}, u32[]{:S(2)}) %collective-permute-start.4) | collective-permute-done | bytes 73760 | tf_op jit(solution)/shard_map/ppermute | solution.py:62
  18.9 0.2 fusion.40
  19.1 0.0 collective-permute-done.1
  19.1 0.2 fusion.2
  19.3 0.1 collective-permute-start.5
  19.4 3.2 %collective-permute-done.5 = f32[16,384]{1,0:T(8,128)S(1)} collective-permute-done((f32[16,384]{1,0:T(8,128)S(1)}, f32[16,384]{1,0:T(8,128)S(1)}, u32[]{:S(2)}, u32[]{:S(2)}) %collective-permute-start.5) | collective-permute-done | bytes 24608 | tf_op jit(solution)/shard_map/ppermute | solution.py:36
  22.6 0.0 collective-permute-start.6
  22.6 3.2 %collective-permute-done.6 = f32[16,384]{1,0:T(8,128)S(1)} collective-permute-done((f32[16,384]{1,0:T(8,128)S(1)}, f32[16,384]{1,0:T(8,128)S(1)}, u32[]{:S(2)}, u32[]{:S(2)}) %collective-permute-start.6) | collective-permute-done | bytes 24608 | tf_op jit(solution)/shard_map/ppermute | solution.py:36
  25.9 0.5 %collective-permute-start.7 = (f32[16,384]{1,0:T(8,128)S(1)}, f32[16,384]{1,0:T(8,128)S(1)}, u32[]{:S(2)}, u32[]{:S(2)}) collective-permute-start(f32[16,384]{1,0:T(8,128)S(1)} %add.385), channel_id=1, source_target_pairs={{0,9},{1,8},{2,11},{3,10},{4,13},{5,12},{6,15},{7,14},{8,1},{9,0},... | collective-permute-start | bytes 73736 | tf_op jit(solution)/shard_map/ppermute | solution.py:36
  26.3 2.8 %collective-permute-done.7 = f32[16,384]{1,0:T(8,128)S(1)} collective-permute-done((f32[16,384]{1,0:T(8,128)S(1)}, f32[16,384]{1,0:T(8,128)S(1)}, u32[]{:S(2)}, u32[]{:S(2)}) %collective-permute-start.7) | collective-permute-done | bytes 24608 | tf_op jit(solution)/shard_map/ppermute | solution.py:36
  29.1 0.5 %collective-permute-start.8 = (f32[16,384]{1,0:T(8,128)S(1)}, f32[16,384]{1,0:T(8,128)S(1)}, u32[]{:S(2)}, u32[]{:S(2)}) collective-permute-start(f32[16,384]{1,0:T(8,128)S(1)} %add.386), channel_id=1, source_target_pairs={{0,17},{1,16},{2,19},{3,18},{4,21},{5,20},{6,23},{7,22},{8,25},{9,... | collective-permute-start | bytes 73736 | tf_op jit(solution)/shard_map/ppermute | solution.py:36
  29.6 3.7 %collective-permute-done.8 = f32[16,384]{1,0:T(8,128)S(1)} collective-permute-done((f32[16,384]{1,0:T(8,128)S(1)}, f32[16,384]{1,0:T(8,128)S(1)}, u32[]{:S(2)}, u32[]{:S(2)}) %collective-permute-start.8) | collective-permute-done | bytes 24608 | tf_op jit(solution)/shard_map/ppermute | solution.py:36
  33.3 0.2 fusion.18
  33.5 0.2 fusion.41
  33.7 0.2 fusion.42
  33.9 0.2 fusion.43
  34.1 0.1 pad_maximum_fusion
  34.2 0.0 collective-permute-start.9
  34.2 1.2 %collective-permute-done.9 = f32[16,192]{1,0:T(8,128)S(1)} collective-permute-done((f32[16,192]{1,0:T(8,128)S(1)}, f32[16,192]{1,0:T(8,128)S(1)}, u32[]{:S(2)}, u32[]{:S(2)}) %collective-permute-start.9) | collective-permute-done | bytes 12320 | tf_op jit(solution)/shard_map/ppermute | solution.py:22
  35.4 0.3 fusion.3
  35.6 0.4 %fusion = f32[16,4,512]{2,0,1:T(8,128)S(1)} fusion(f32[6,6,4,512]{3,1,0,2:T(8,128)S(1)} %fusion.17, f32[16,4,6,6]{0,3,2,1:T(8,128)S(1)} %reshape.219, f32[16,4,512]{2,1,0:T(4,128)S(1)} %copy-done.1), kind=kOutput, calls=%fused_computation.1 | convolution fusion | flops 14188544 | bytes 566272 | tf_op jit(solution)/shard_map/rsdk,dksm->rsm/dot_general | solution.py:124
  36.1 0.7 %copy.38 = f32[16,4,512]{2,1,0:T(4,128)} copy(f32[16,4,512]{2,0,1:T(8,128)S(1)} %fusion) | data formatting | bytes 262144 | tf_op jit(solution)/shard_map/sub | solution.py:124
  (19 shorter events, 0.3 us)
Async XLA Ops:
  0.0 0.7 %copy-start.5 = (s32[128,6]{0,1:T(8,128)S(1)}, s32[128,6]{0,1:T(8,128)}, u32[]{:S(2)}) copy-start(s32[128,6]{0,1:T(8,128)} %param.12) | copy-start | bytes 9220
  0.0 1.6 %copy-start.3 = (f32[6,4,512]{2,1,0:T(4,128)S(1)}, f32[6,4,512]{2,1,0:T(4,128)}, u32[]{:S(2)}) copy-start(f32[6,4,512]{2,1,0:T(4,128)} %param.9) | copy-start | bytes 147460
  0.8 0.7 %copy-start.4 = (s32[4,512]{1,0:T(4,128)S(1)}, s32[4,512]{1,0:T(4,128)}, u32[]{:S(2)}) copy-start(s32[4,512]{1,0:T(4,128)} %param.11) | copy-start | bytes 24580
  1.6 0.8 %copy-start = (f32[6,4,512]{2,1,0:T(4,128)S(1)}, f32[6,4,512]{2,1,0:T(4,128)}, u32[]{:S(2)}) copy-start(f32[6,4,512]{2,1,0:T(4,128)} %param.10) | copy-start | bytes 147460
  2.5 0.9 %copy-start.1 = (f32[16,4,512]{2,1,0:T(4,128)S(1)}, f32[16,4,512]{2,1,0:T(4,128)}, u32[]{:S(2)}) copy-start(f32[16,4,512]{2,1,0:T(4,128)} %param.8) | copy-start | bytes 393220
  3.9 0.7 %copy-start.6 = (s32[6]{0:T(128)S(1)}, s32[6]{0:T(128)}, u32[]{:S(2)}) copy-start(s32[6]{0:T(128)} %constant.127.clone) | copy-start | bytes 76
  3.9 0.7 %copy-start.7 = (s32[6]{0:T(128)S(1)}, s32[6]{0:T(128)}, u32[]{:S(2)}) copy-start(s32[6]{0:T(128)} %constant.132) | copy-start | bytes 76
  4.0 1.8 %copy-start.2 = (f32[48,384]{1,0:T(8,128)S(1)}, f32[48,384]{1,0:T(8,128)}, u32[]{:S(2)}) copy-start(f32[48,384]{1,0:T(8,128)} %param.13) | copy-start | bytes 221188
  5.2 7.8 %collective-permute-start = (f32[16,192]{1,0:T(8,128)S(1)}, f32[16,192]{1,0:T(8,128)S(1)}, u32[]{:S(2)}, u32[]{:S(2)}) collective-permute-start(f32[16,192]{1,0:T(8,128)S(1)} %fusion.4), channel_id=1, source_target_pairs={{0,1},{1,0},{2,3},{3,2},{4,5},{5,4},{6,7},{7,6},{8,9},{9,8},{10,11... | collective-permute-start | bytes 36872 | tf_op jit(solution)/shard_map/ppermute | solution.py:22
  5.7 8.1 %collective-permute-start.2 = (f32[48,384]{1,0:T(8,128)S(1)}, f32[48,384]{1,0:T(8,128)S(1)}, u32[]{:S(2)}, u32[]{:S(2)}) collective-permute-start(f32[48,384]{1,0:T(8,128)S(1)} %copy-done.2), channel_id=1, source_target_pairs={{16,0},{17,1},{19,2},{18,3},{21,4},{20,5},{22,6},{23,7},{25,8},{24... | collective-permute-start | bytes 221192 | tf_op jit(solution)/shard_map/ppermute | solution.py:62
  9.4 5.5 %collective-permute-start.3 = (f32[48,384]{1,0:T(8,128)S(1)}, f32[48,384]{1,0:T(8,128)S(1)}, u32[]{:S(2)}, u32[]{:S(2)}) collective-permute-start(f32[48,384]{1,0:T(8,128)S(1)} %copy-done.2), channel_id=1, source_target_pairs={{2,0},{3,1},{5,2},{4,3},{7,4},{6,5},{8,6},{9,7},{11,8},{10,9},{12,... | collective-permute-start | bytes 221192 | tf_op jit(solution)/shard_map/ppermute | solution.py:62
  12.6 6.3 %collective-permute-start.4 = (f32[48,384]{1,0:T(8,128)S(1)}, f32[48,384]{1,0:T(8,128)S(1)}, u32[]{:S(2)}, u32[]{:S(2)}) collective-permute-start(f32[48,384]{1,0:T(8,128)S(1)} %copy-done.2), channel_id=1, source_target_pairs={{14,0},{15,1},{1,2},{0,3},{3,4},{2,5},{4,6},{5,7},{7,8},{6,9},{8,1... | collective-permute-start | bytes 221192 | tf_op jit(solution)/shard_map/ppermute | solution.py:62
  12.6 6.5 %collective-permute-start.1 = (f32[48,384]{1,0:T(8,128)S(1)}, f32[48,384]{1,0:T(8,128)S(1)}, u32[]{:S(2)}, u32[]{:S(2)}) collective-permute-start(f32[48,384]{1,0:T(8,128)S(1)} %copy-done.2), channel_id=1, source_target_pairs={{0,1},{1,0},{2,3},{3,2},{4,5},{5,4},{6,7},{7,6},{8,9},{9,8},{10,11... | collective-permute-start | bytes 221192 | tf_op jit(solution)/shard_map/ppermute | solution.py:66
  19.3 3.3 %collective-permute-start.5 = (f32[16,384]{1,0:T(8,128)S(1)}, f32[16,384]{1,0:T(8,128)S(1)}, u32[]{:S(2)}, u32[]{:S(2)}) collective-permute-start(f32[16,384]{1,0:T(8,128)S(1)} %fusion.2), channel_id=1, source_target_pairs={{0,3},{1,2},{2,1},{3,0},{4,7},{5,6},{6,5},{7,4},{8,11},{9,10},{10,... | collective-permute-start | bytes 73736 | tf_op jit(solution)/shard_map/ppermute | solution.py:36
  22.6 3.3 %collective-permute-start.6 = (f32[16,384]{1,0:T(8,128)S(1)}, f32[16,384]{1,0:T(8,128)S(1)}, u32[]{:S(2)}, u32[]{:S(2)}) collective-permute-start(f32[16,384]{1,0:T(8,128)S(1)} %add.384), channel_id=1, source_target_pairs={{0,5},{1,4},{2,7},{3,6},{4,1},{5,0},{6,3},{7,2},{8,13},{9,12},{10,... | collective-permute-start | bytes 73736 | tf_op jit(solution)/shard_map/ppermute | solution.py:36
  25.9 3.3 %collective-permute-start.7 = (f32[16,384]{1,0:T(8,128)S(1)}, f32[16,384]{1,0:T(8,128)S(1)}, u32[]{:S(2)}, u32[]{:S(2)}) collective-permute-start(f32[16,384]{1,0:T(8,128)S(1)} %add.385), channel_id=1, source_target_pairs={{0,9},{1,8},{2,11},{3,10},{4,13},{5,12},{6,15},{7,14},{8,1},{9,0},... | collective-permute-start | bytes 73736 | tf_op jit(solution)/shard_map/ppermute | solution.py:36
  29.1 4.2 %collective-permute-start.8 = (f32[16,384]{1,0:T(8,128)S(1)}, f32[16,384]{1,0:T(8,128)S(1)}, u32[]{:S(2)}, u32[]{:S(2)}) collective-permute-start(f32[16,384]{1,0:T(8,128)S(1)} %add.386), channel_id=1, source_target_pairs={{0,17},{1,16},{2,19},{3,18},{4,21},{5,20},{6,23},{7,22},{8,25},{9,... | collective-permute-start | bytes 73736 | tf_op jit(solution)/shard_map/ppermute | solution.py:36
  34.2 1.2 %collective-permute-start.9 = (f32[16,192]{1,0:T(8,128)S(1)}, f32[16,192]{1,0:T(8,128)S(1)}, u32[]{:S(2)}, u32[]{:S(2)}) collective-permute-start(f32[16,192]{1,0:T(8,128)S(1)} %pad_maximum_fusion), channel_id=1, source_target_pairs={{0,1},{1,0},{2,3},{3,2},{4,5},{5,4},{6,7},{7,6},{8,9},{9,8},{10,11... | collective-permute-start | bytes 36872 | tf_op jit(solution)/shard_map/ppermute | solution.py:22
where the time goes:
time: 37.1 us; the launch traced here: 36.8 us
  waiting for transfers between devices  19.6 us (53%)
  starting transfers between devices  8.8 us (24%)
  local copies, waits for them, and re-layouts  4.62 us (12%)
  matrix products  2.88 us (8%)
  other arithmetic  0.63 us (2%)
    ppermute x4, waiting for transfers between devices, crossed_sum(): value = value + lax.ppermute(value, ('sub', 'crs'), pairs)  12.9 us
    ppermute x3, starting transfers between devices, fetched(): return lax.ppermute(coarse_factor, ('sub', 'crs'), pairs)  6.87 us
    ppermute x3, waiting for transfers between devices, fetched(): return lax.ppermute(coarse_factor, ('sub', 'crs'), pairs)  5.51 us
    unnamed x17, local copies, waits for them, and re-layouts  3.55 us
    ppermute x2, waiting for transfers between devices, all_sum(): lax.ppermute(value, axis, [(i, i ^ step) for i in range(peers)])  1.17 us
    ppermute x4, starting transfers between devices, crossed_sum(): value = value + lax.ppermute(value, ('sub', 'crs'), pairs)  1.02 us
    dot_general x4, matrix products, body(): jnp.einsum('rp,cp->rc', panel, f, precision=HIGHEST)  0.75 us
    sub x1, local copies, waits for them, and re-layouts, body(): multipliers - jnp.einsum('rsdk,dksm->rsm', near, rows, precision=HIGHEST)  0.74 us
  transfers between devices with their start and end apart: 10, of which 8 were waited for; matrix products, arithmetic and copies ran while one was open for 2% of the time, Pallas kernels for 0%

commit v1 on v0

--- a/solution.py
+++ b/solution.py
@@ -1,6 +1,8 @@
 import jax
 import jax.numpy as jnp
 from jax import lax
+from jax.experimental import pallas as pl
+from jax.experimental.pallas import tpu as pltpu
 from jax.sharding import PartitionSpec as P
 
 
@@ -36,6 +38,18 @@
         value = value + lax.ppermute(value, ("sub", "crs"), pairs)
         step *= 2
     return value
+
+
+def split_rows(face_dir, own, neighbour, face, rows):
+    for s in range(rows.shape[0]):
+        points = face[s : s + 1, :]
+        toward = jnp.zeros_like(points)
+        for f in range(NFACE):
+            toward = jnp.where(points == f, face_dir[s, f], toward)
+        near = neighbour[:, s, :]
+        rows[s, 0] = own[:, s, :]
+        for d in range(1, NDIR):
+            rows[s, d] = jnp.where(toward == d, near, 0.0)
 
 
 def body(multipliers, own_modes, neighbour_modes, face_index, neighbour_list, coarse_factor):
@@ -91,19 +105,23 @@
     face_dir = jnp.zeros_like(local_nbrs)
     for which in range(NDIR - 2, -1, -1):
         face_dir = jnp.where(local_nbrs == across[which][:, None], which + 1, face_dir)
-    point_dir = jnp.zeros_like(face_index)
-    for which_face in range(NFACE):
-        point_dir = jnp.where(
-            face_index == which_face, face_dir[:, which_face : which_face + 1], point_dir
-        )
-    rows = [own_modes]
-    for which in range(1, NDIR):
-        rows.append(jnp.where((point_dir == which)[None], neighbour_modes, 0.0))
-    rows = jnp.stack(rows)
-    sums = jnp.einsum("dksm,rsm->rsdk", rows, multipliers, precision=HIGHEST)
+    rows = pl.pallas_call(
+        split_rows,
+        out_shape=pltpu.VMEM((local_subs, NDIR, MODES, face_index.shape[1]), jnp.float32),
+        in_specs=[
+            pl.BlockSpec(memory_space=pltpu.SMEM),
+            pl.BlockSpec(memory_space=pltpu.VMEM),
+            pl.BlockSpec(memory_space=pltpu.VMEM),
+            pl.BlockSpec(memory_space=pltpu.VMEM),
+        ],
+        out_specs=pl.BlockSpec(memory_space=pltpu.VMEM),
+        name="split_rows",
+    )(face_dir, own_modes, neighbour_modes, face_index)
+    sums = jnp.einsum("sdkm,rsm->rsdk", rows, multipliers, precision=HIGHEST)
 
-    blocks = jnp.array([0, 1, 2, 3, 0, 0], jnp.int32)
-    moves = jnp.array([0, 0, 0, 0, 1, group_subs - 1], jnp.int32)
+    ways = lax.iota(jnp.int32, NDIR)
+    blocks = jnp.where(ways < NBLOCK, ways, 0)
+    moves = jnp.where(ways == 4, 1, jnp.where(ways == 5, group_subs - 1, 0))
     target_sub = (third[:, None] + moves[None]) % group_subs
     target = (blocks[None] * group_subs + target_sub)[:, :, None] * MODES + lax.iota(jnp.int32, MODES)
     wide = NBLOCK * group_subs * MODES
@@ -121,7 +139,7 @@
     amps = all_sum(amps, "crs")
     near = jnp.einsum("rw,nw->rn", amps, chosen, precision=HIGHEST)
     near = near.reshape(width_rhs, local_subs, NDIR, MODES)
-    return multipliers - jnp.einsum("rsdk,dksm->rsm", near, rows, precision=HIGHEST)
+    return multipliers - jnp.einsum("rsdk,sdkm->rsm", near, rows, precision=HIGHEST)
 
 
 def solution(mesh):

time: 37.1 us -> 36.3 us (0.978)
  local copies, waits for them, and re-layouts: 4.62 us -> 1.76 us
  waiting for transfers between devices: 19.6 us -> 21 us
  Pallas kernels: 0 us -> 0.94 us
  starting transfers between devices: 8.8 us -> 8.36 us
    unnamed x17 -> x7, local copies, waits for them, and re-layouts: 3.55 us -> 0.71 us
    ppermute x4, waiting for transfers between devices: 12.9 us -> 14.4 us  [crossed_sum(): value = value + lax.ppermute(value, ('sub', 'crs'), pairs)]
    pallas_call x0 -> x1, Pallas kernels: none -> 0.94 us  [body(): pl.pallas_call(split_rows, out_shape=pltpu.VMEM((local_subs, NDIR, MODES,...]
    ppermute x4, starting transfers between devices: 1.02 us -> 0.23 us  [crossed_sum(): value = value + lax.ppermute(value, ('sub', 'crs'), pairs)]
    select_n x1, other arithmetic: 0.08 us -> 0.65 us  [body(): jnp.where(local_nbrs == across[which][:, None], which + 1, face_dir)]
where the time goes in v1:
time: 36.3 us; the launch traced here: 36.1 us
  waiting for transfers between devices  21 us (58%)
  starting transfers between devices  8.36 us (23%)
  matrix products  2.9 us (8%)
  local copies, waits for them, and re-layouts  1.76 us (5%)
  other arithmetic  1 us (3%)
  Pallas kernels  0.94 us (3%)
    ppermute x4, waiting for transfers between devices, crossed_sum(): value = value + lax.ppermute(value, ('sub', 'crs'), pairs)  14.4 us
    ppermute x3, starting transfers between devices, fetched(): return lax.ppermute(coarse_factor, ('sub', 'crs'), pairs)  6.87 us
    ppermute x3, waiting for transfers between devices, fetched(): return lax.ppermute(coarse_factor, ('sub', 'crs'), pairs)  5.51 us
    ppermute x2, waiting for transfers between devices, all_sum(): lax.ppermute(value, axis, [(i, i ^ step) for i in range(peers)])  1.07 us
    pallas_call x1, Pallas kernels, body(): pl.pallas_call(split_rows, out_shape=pltpu.VMEM((local_subs, NDIR, MODES,...  0.94 us
    dot_general x4, matrix products, body(): jnp.einsum('rp,cp->rc', panel, f, precision=HIGHEST)  0.75 us
    sub x1, local copies, waits for them, and re-layouts, body(): multipliers - jnp.einsum('rsdk,sdkm->rsm', near, rows, precision=HIGHEST)  0.74 us
  transfers between devices with their start and end apart: 10, of which 8 were waited for; matrix products, arithmetic and copies ran while one was open for 2% of the time, Pallas kernels for 0%

profile of v1, /device:TPU:0, one launch (start us, length us, event | category | flops | bytes accessed | tf_op | source)
XLA Modules:
  0.0 36.1 jit_solution(12062194158003446185)
XLA Ops:
  0.0 0.0 copy-start
  0.1 0.6 %copy-done = s32[128,6]{0,1:T(8,128)S(1)} copy-done((s32[128,6]{0,1:T(8,128)S(1)}, s32[128,6]{0,1:T(8,128)}, u32[]{:S(2)}) %copy-start) | copy-done | bytes 3096
  0.7 0.1 constant_dynamic-slice_fusion
  0.8 0.1 copy.22
  0.9 0.7 %select_select_fusion.face_dir = s32[4,6]{1,0:T(4,128)} fusion(s32[4,6]{1,0:T(4,128)S(1)} %copy.22, s32[4]{0:T(128)S(1)} %get-tuple-element.11, s32[4]{0:T(128)S(1)} %get-tuple-element.10, s32[4]{0:T(128)S(1)} %get-tuple-element.12, s32[4]{0:T(128)S(1)} %get-tuple-element.13, s32[4]{0:T(128)S(1)} %get-tuple-element.14), kind=kLoop, calls=%fused_computation.38 | loop fusion | flops 240 | bytes 272 | tf_op jit(solution)/shard_map/jit(_where)/select_n | solution.py:107
  1.5 0.0 copy-start.1
  1.5 0.9 %split_rows.1 = f32[4,6,6,512]{3,2,1,0:T(8,128)S(1)} custom-call(s32[4,6]{1,0:T(4,128)} %select_select_fusion.face_dir, f32[6,4,512]{2,1,0:T(4,128)} %own.1, f32[6,4,512]{2,1,0:T(4,128)} %neighbour.1, s32[4,512]{1,0:T(4,128)} %face.1), custom_call_target="tpu_custom_call" | custom-call | tf_op jit(solution)/shard_map/split_rows/pallas_call | solution.py:108
  2.5 0.0 copy-done.1
  2.5 0.6 %convolution_bitcast_fusion.1 = f32[16,4,6,6]{0,3,2,1:T(8,128)S(1)} fusion(f32[4,6,6,512]{3,2,1,0:T(8,128)S(1)} %split_rows.1, f32[16,4,512,1]{2,1,0,3:T(4,128)S(1)} %bitcast.36), kind=kOutput, calls=%fused_computation.2 | convolution fusion | flops 14155776 | bytes 435200 | tf_op jit(solution)/shard_map/sdkm,rsm->rsdk/dot_general | solution.py:120
  3.1 0.0 copy-start.2
  3.1 0.1 fusion.11
  3.1 0.1 iota_add_fusion
  3.2 0.1 add.378
  3.3 0.3 fusion.4
  3.6 0.5 %collective-permute-start = (f32[16,192]{1,0:T(8,128)S(1)}, f32[16,192]{1,0:T(8,128)S(1)}, u32[]{:S(2)}, u32[]{:S(2)}) collective-permute-start(f32[16,192]{1,0:T(8,128)S(1)} %fusion.4), channel_id=1, source_target_pairs={{0,1},{1,0},{2,3},{3,2},{4,5},{5,4},{6,7},{7,6},{8,9},{9,8},{10,11... | collective-permute-start | bytes 36872 | tf_op jit(solution)/shard_map/ppermute | solution.py:24
  4.1 0.0 copy-done.2
  4.1 3.7 %collective-permute-start.2 = (f32[48,384]{1,0:T(8,128)S(1)}, f32[48,384]{1,0:T(8,128)S(1)}, u32[]{:S(2)}, u32[]{:S(2)}) collective-permute-start(f32[48,384]{1,0:T(8,128)S(1)} %copy-done.2), channel_id=1, source_target_pairs={{16,0},{17,1},{19,2},{18,3},{21,4},{20,5},{22,6},{23,7},{25,8},{24... | collective-permute-start | bytes 221192 | tf_op jit(solution)/shard_map/ppermute | solution.py:76
  7.8 3.2 %collective-permute-start.3 = (f32[48,384]{1,0:T(8,128)S(1)}, f32[48,384]{1,0:T(8,128)S(1)}, u32[]{:S(2)}, u32[]{:S(2)}) collective-permute-start(f32[48,384]{1,0:T(8,128)S(1)} %copy-done.2), channel_id=1, source_target_pairs={{2,0},{3,1},{5,2},{4,3},{7,4},{6,5},{8,6},{9,7},{11,8},{10,9},{12,... | collective-permute-start | bytes 221192 | tf_op jit(solution)/shard_map/ppermute | solution.py:76
  11.0 0.0 collective-permute-start.4
  11.0 0.6 %collective-permute-start.1 = (f32[48,384]{1,0:T(8,128)S(1)}, f32[48,384]{1,0:T(8,128)S(1)}, u32[]{:S(2)}, u32[]{:S(2)}) collective-permute-start(f32[48,384]{1,0:T(8,128)S(1)} %copy-done.2), channel_id=1, source_target_pairs={{0,1},{1,0},{2,3},{3,2},{4,5},{5,4},{6,7},{7,6},{8,9},{9,8},{10,11... | collective-permute-start | bytes 221192 | tf_op jit(solution)/shard_map/ppermute | solution.py:80
  11.6 0.0 collective-permute-done
  11.6 0.1 reshape.230
  11.7 0.5 %collective-permute-done.2 = f32[48,384]{1,0:T(8,128)S(1)} collective-permute-done((f32[48,384]{1,0:T(8,128)S(1)}, f32[48,384]{1,0:T(8,128)S(1)}, u32[]{:S(2)}, u32[]{:S(2)}) %collective-permute-start.2) | collective-permute-done | bytes 73760 | tf_op jit(solution)/shard_map/ppermute | solution.py:76
  12.2 0.2 fusion.29
  12.4 1.2 %collective-permute-done.3 = f32[48,384]{1,0:T(8,128)S(1)} collective-permute-done((f32[48,384]{1,0:T(8,128)S(1)}, f32[48,384]{1,0:T(8,128)S(1)}, u32[]{:S(2)}, u32[]{:S(2)}) %collective-permute-start.3) | collective-permute-done | bytes 73760 | tf_op jit(solution)/shard_map/ppermute | solution.py:76
  13.6 0.2 fusion.30
  13.8 3.8 %collective-permute-done.4 = f32[48,384]{1,0:T(8,128)S(1)} collective-permute-done((f32[48,384]{1,0:T(8,128)S(1)}, f32[48,384]{1,0:T(8,128)S(1)}, u32[]{:S(2)}, u32[]{:S(2)}) %collective-permute-start.4) | collective-permute-done | bytes 73760 | tf_op jit(solution)/shard_map/ppermute | solution.py:76
  17.6 0.2 fusion.31
  17.7 0.0 collective-permute-done.1
  17.7 0.2 fusion.2
  17.9 0.1 collective-permute-start.5
  18.0 3.4 %collective-permute-done.5 = f32[16,384]{1,0:T(8,128)S(1)} collective-permute-done((f32[16,384]{1,0:T(8,128)S(1)}, f32[16,384]{1,0:T(8,128)S(1)}, u32[]{:S(2)}, u32[]{:S(2)}) %collective-permute-start.5) | collective-permute-done | bytes 24608 | tf_op jit(solution)/shard_map/ppermute | solution.py:38
  21.4 0.0 collective-permute-start.6
  21.4 3.3 %collective-permute-done.6 = f32[16,384]{1,0:T(8,128)S(1)} collective-permute-done((f32[16,384]{1,0:T(8,128)S(1)}, f32[16,384]{1,0:T(8,128)S(1)}, u32[]{:S(2)}, u32[]{:S(2)}) %collective-permute-start.6) | collective-permute-done | bytes 24608 | tf_op jit(solution)/shard_map/ppermute | solution.py:38
  24.7 0.0 collective-permute-start.7
  24.7 3.2 %collective-permute-done.7 = f32[16,384]{1,0:T(8,128)S(1)} collective-permute-done((f32[16,384]{1,0:T(8,128)S(1)}, f32[16,384]{1,0:T(8,128)S(1)}, u32[]{:S(2)}, u32[]{:S(2)}) %collective-permute-start.7) | collective-permute-done | bytes 24608 | tf_op jit(solution)/shard_map/ppermute | solution.py:38
  28.0 0.1 collective-permute-start.8
  28.1 4.4 %collective-permute-done.8 = f32[16,384]{1,0:T(8,128)S(1)} collective-permute-done((f32[16,384]{1,0:T(8,128)S(1)}, f32[16,384]{1,0:T(8,128)S(1)}, u32[]{:S(2)}, u32[]{:S(2)}) %collective-permute-start.8) | collective-permute-done | bytes 24608 | tf_op jit(solution)/shard_map/ppermute | solution.py:38
  32.5 0.2 fusion.8
  32.7 0.2 fusion.32
  32.9 0.2 fusion.33
  33.1 0.2 fusion.34
  33.3 0.1 pad_maximum_fusion
  33.4 0.1 collective-permute-start.9
  33.5 1.1 %collective-permute-done.9 = f32[16,192]{1,0:T(8,128)S(1)} collective-permute-done((f32[16,192]{1,0:T(8,128)S(1)}, f32[16,192]{1,0:T(8,128)S(1)}, u32[]{:S(2)}, u32[]{:S(2)}) %collective-permute-start.9) | collective-permute-done | bytes 12320 | tf_op jit(solution)/shard_map/ppermute | solution.py:24
  34.6 0.3 fusion.3
  34.9 0.4 %fusion = f32[16,4,512]{2,0,1:T(8,128)S(1)} fusion(f32[4,6,6,512]{3,2,1,0:T(8,128)S(1)} %split_rows.1, f32[16,4,6,6]{0,3,2,1:T(8,128)S(1)} %reshape.231, f32[16,4,512]{2,1,0:T(4,128)S(1)} %copy-done.1), kind=kOutput, calls=%fused_computation.1 | convolution fusion | flops 14188544 | bytes 566272 | tf_op jit(solution)/shard_map/rsdk,sdkm->rsm/dot_general | solution.py:142
  35.3 0.7 %copy.16 = f32[16,4,512]{2,1,0:T(4,128)} copy(f32[16,4,512]{2,0,1:T(8,128)S(1)} %fusion) | data formatting | bytes 262144 | tf_op jit(solution)/shard_map/sub | solution.py:142
  (12 shorter events, 0.2 us)
Async XLA Ops:
  0.0 0.7 %copy-start = (s32[128,6]{0,1:T(8,128)S(1)}, s32[128,6]{0,1:T(8,128)}, u32[]{:S(2)}) copy-start(s32[128,6]{0,1:T(8,128)} %param.10) | copy-start | bytes 9220
  1.5 1.0 %copy-start.1 = (f32[16,4,512]{2,1,0:T(4,128)S(1)}, f32[16,4,512]{2,1,0:T(4,128)}, u32[]{:S(2)}) copy-start(f32[16,4,512]{2,1,0:T(4,128)} %param.6) | copy-start | bytes 393220
  3.1 1.1 %copy-start.2 = (f32[48,384]{1,0:T(8,128)S(1)}, f32[48,384]{1,0:T(8,128)}, u32[]{:S(2)}) copy-start(f32[48,384]{1,0:T(8,128)} %param.11) | copy-start | bytes 221188
  3.6 8.0 %collective-permute-start = (f32[16,192]{1,0:T(8,128)S(1)}, f32[16,192]{1,0:T(8,128)S(1)}, u32[]{:S(2)}, u32[]{:S(2)}) collective-permute-start(f32[16,192]{1,0:T(8,128)S(1)} %fusion.4), channel_id=1, source_target_pairs={{0,1},{1,0},{2,3},{3,2},{4,5},{5,4},{6,7},{7,6},{8,9},{9,8},{10,11... | collective-permute-start | bytes 36872 | tf_op jit(solution)/shard_map/ppermute | solution.py:24
  4.1 8.1 %collective-permute-start.2 = (f32[48,384]{1,0:T(8,128)S(1)}, f32[48,384]{1,0:T(8,128)S(1)}, u32[]{:S(2)}, u32[]{:S(2)}) collective-permute-start(f32[48,384]{1,0:T(8,128)S(1)} %copy-done.2), channel_id=1, source_target_pairs={{16,0},{17,1},{19,2},{18,3},{21,4},{20,5},{22,6},{23,7},{25,8},{24... | collective-permute-start | bytes 221192 | tf_op jit(solution)/shard_map/ppermute | solution.py:76
  7.8 5.8 %collective-permute-start.3 = (f32[48,384]{1,0:T(8,128)S(1)}, f32[48,384]{1,0:T(8,128)S(1)}, u32[]{:S(2)}, u32[]{:S(2)}) collective-permute-start(f32[48,384]{1,0:T(8,128)S(1)} %copy-done.2), channel_id=1, source_target_pairs={{2,0},{3,1},{5,2},{4,3},{7,4},{6,5},{8,6},{9,7},{11,8},{10,9},{12,... | collective-permute-start | bytes 221192 | tf_op jit(solution)/shard_map/ppermute | solution.py:76
  11.0 6.6 %collective-permute-start.4 = (f32[48,384]{1,0:T(8,128)S(1)}, f32[48,384]{1,0:T(8,128)S(1)}, u32[]{:S(2)}, u32[]{:S(2)}) collective-permute-start(f32[48,384]{1,0:T(8,128)S(1)} %copy-done.2), channel_id=1, source_target_pairs={{14,0},{15,1},{1,2},{0,3},{3,4},{2,5},{4,6},{5,7},{7,8},{6,9},{8,1... | collective-permute-start | bytes 221192 | tf_op jit(solution)/shard_map/ppermute | solution.py:76
  11.0 6.7 %collective-permute-start.1 = (f32[48,384]{1,0:T(8,128)S(1)}, f32[48,384]{1,0:T(8,128)S(1)}, u32[]{:S(2)}, u32[]{:S(2)}) collective-permute-start(f32[48,384]{1,0:T(8,128)S(1)} %copy-done.2), channel_id=1, source_target_pairs={{0,1},{1,0},{2,3},{3,2},{4,5},{5,4},{6,7},{7,6},{8,9},{9,8},{10,11... | collective-permute-start | bytes 221192 | tf_op jit(solution)/shard_map/ppermute | solution.py:80
  17.9 3.5 %collective-permute-start.5 = (f32[16,384]{1,0:T(8,128)S(1)}, f32[16,384]{1,0:T(8,128)S(1)}, u32[]{:S(2)}, u32[]{:S(2)}) collective-permute-start(f32[16,384]{1,0:T(8,128)S(1)} %fusion.2), channel_id=1, source_target_pairs={{0,3},{1,2},{2,1},{3,0},{4,7},{5,6},{6,5},{7,4},{8,11},{9,10},{10,... | collective-permute-start | bytes 73736 | tf_op jit(solution)/shard_map/ppermute | solution.py:38
  21.4 3.3 %collective-permute-start.6 = (f32[16,384]{1,0:T(8,128)S(1)}, f32[16,384]{1,0:T(8,128)S(1)}, u32[]{:S(2)}, u32[]{:S(2)}) collective-permute-start(f32[16,384]{1,0:T(8,128)S(1)} %add.384), channel_id=1, source_target_pairs={{0,5},{1,4},{2,7},{3,6},{4,1},{5,0},{6,3},{7,2},{8,13},{9,12},{10,... | collective-permute-start | bytes 73736 | tf_op jit(solution)/shard_map/ppermute | solution.py:38
  24.7 3.3 %collective-permute-start.7 = (f32[16,384]{1,0:T(8,128)S(1)}, f32[16,384]{1,0:T(8,128)S(1)}, u32[]{:S(2)}, u32[]{:S(2)}) collective-permute-start(f32[16,384]{1,0:T(8,128)S(1)} %add.385), channel_id=1, source_target_pairs={{0,9},{1,8},{2,11},{3,10},{4,13},{5,12},{6,15},{7,14},{8,1},{9,0},... | collective-permute-start | bytes 73736 | tf_op jit(solution)/shard_map/ppermute | solution.py:38
  28.0 4.6 %collective-permute-start.8 = (f32[16,384]{1,0:T(8,128)S(1)}, f32[16,384]{1,0:T(8,128)S(1)}, u32[]{:S(2)}, u32[]{:S(2)}) collective-permute-start(f32[16,384]{1,0:T(8,128)S(1)} %add.386), channel_id=1, source_target_pairs={{0,17},{1,16},{2,19},{3,18},{4,21},{5,20},{6,23},{7,22},{8,25},{9,... | collective-permute-start | bytes 73736 | tf_op jit(solution)/shard_map/ppermute | solution.py:38
  33.4 1.2 %collective-permute-start.9 = (f32[16,192]{1,0:T(8,128)S(1)}, f32[16,192]{1,0:T(8,128)S(1)}, u32[]{:S(2)}, u32[]{:S(2)}) collective-permute-start(f32[16,192]{1,0:T(8,128)S(1)} %pad_maximum_fusion), channel_id=1, source_target_pairs={{0,1},{1,0},{2,3},{3,2},{4,5},{5,4},{6,7},{7,6},{8,9},{9,8},{10,11... | collective-permute-start | bytes 36872 | tf_op jit(solution)/shard_map/ppermute | solution.py:24
